TPU v7x, 32 devices: a whole 2x2x4 slice. The times are simulated.
32 devices in a mesh: ang: 16 (over z, y, core), sl: 2 (over x).
Axes of the slice: x: 2, y: 2, z: 4, core: 2. Of those that a mesh axis runs over, the one named last changes fastest.
Arguments:
- sinogram: bfloat16 [16, 32, 1024], P('sl', 'ang'), may hold values from -72 to 72
- detector_coord: int32 [32, 32, 512], P('ang', 'sl'), may hold values from 0 to 1072693247
Outputs:
- image_rows: float32 [32, 16, 512], P('ang', 'sl')
All inputs are finite; a program needn't handle non-finite values.
Results may differ from a plain program's by a relative error of at most 0.0052.
Values may be sent and summed in bfloat16 or wider, within the bound.
A program may use at most 64 MiB of HBM per device.

v0:
```python
import math

import jax
import jax.numpy as jnp
from jax import lax
from jax.sharding import PartitionSpec as P


def ramp_table(bin_count):
    first = lax.broadcasted_iota(jnp.int32, (bin_count, bin_count), 0)
    second = lax.broadcasted_iota(jnp.int32, (bin_count, bin_count), 1)
    offset = second - first
    offset_sq = jnp.maximum((offset * offset).astype(jnp.float32), jnp.float32(1.0))
    odd_mask = offset % 2 != 0
    values = jnp.where(
        offset == 0,
        jnp.float32(0.25),
        jnp.where(odd_mask, jnp.float32(-1.0 / math.pi**2) / offset_sq, jnp.float32(0.0)),
    )
    return values.astype(jnp.bfloat16)


def dense_weights(row_coords, bin_count):
    bin_left = row_coords // 1048576
    fraction = (row_coords % 1048576).astype(jnp.float32) / jnp.float32(1048576.0)
    positions = lax.broadcasted_iota(jnp.int32, row_coords.shape + (bin_count,), row_coords.ndim)
    left_part = jnp.where(
        positions == bin_left[..., None], 1.0 - fraction[..., None], jnp.float32(0.0)
    )
    right_part = jnp.where(
        positions == bin_left[..., None] + 1, fraction[..., None], jnp.float32(0.0)
    )
    return (left_part + right_part).astype(jnp.bfloat16)


def project_block(coords_block, projections):
    weights = dense_weights(coords_block, projections.shape[2])
    return jnp.einsum("arxb,sab->rsx", weights, projections, preferred_element_type=jnp.float32)


def shards(sinogram, detector_coord):
    slices, angles, bin_count = sinogram.shape
    width_pixels = detector_coord.shape[2]
    table = ramp_table(bin_count)
    filtered = jnp.dot(
        sinogram.reshape(slices * angles, bin_count), table, preferred_element_type=jnp.float32
    )
    filtered = filtered.astype(jnp.bfloat16).reshape(slices, angles, bin_count)
    fbp_scale = jnp.float32(math.pi / (angles * lax.axis_size("ang")))
    coord_table = lax.all_gather(detector_coord, "sl", axis=1, tiled=True)
    row_share = coord_table.shape[1] // lax.axis_size("ang")
    own_rows = lax.all_to_all(coord_table, "ang", split_axis=1, concat_axis=0, tiled=True)
    start_value = jnp.zeros((row_share, slices, width_pixels), jnp.float32)
    shard_piece = lax.all_gather(filtered, "ang", axis=1, tiled=True)
    group_count = shard_piece.shape[1] // angles

    def one_group(group_step, inner):
        coords_block = lax.dynamic_slice_in_dim(own_rows, group_step * angles, angles, 0)
        projections = lax.dynamic_slice_in_dim(shard_piece, group_step * angles, angles, 1)
        return inner + project_block(coords_block, projections)

    summed = lax.fori_loop(0, group_count, one_group, start_value)
    image_rows = summed * fbp_scale
    return image_rows


def solution(mesh):
    in_specs = (P("sl", "ang", None), P("ang", "sl", None))
    out_specs = P("ang", "sl", None)
    return jax.shard_map(shards, mesh=mesh, in_specs=in_specs, out_specs=out_specs, check_vma=False)
```

profile of v0, /device:TPU:0, one launch (start us, length us, event | category | flops | bytes accessed | tf_op | source)
XLA Modules:
  0.0 78.2 jit_solution(12581759351553760365)
XLA Ops:
  0.0 0.0 copy-start
  0.0 0.9 %copy.9 = s32[2,16,512]{2,0,1:T(2,128)S(1)} copy(s32[2,16,512]{2,1,0:T(8,128)} %param.5) | data formatting | bytes 131072 | tf_op args[1]
  0.9 6.0 %all_gather.7 = s32[2,32,512]{2,0,1:T(2,128)} all-gather(s32[2,16,512]{2,0,1:T(2,128)S(1)} %copy.9), channel_id=1, replica_groups=mesh['ang'=16,'sl'=2] {'sl'}, dimensions={1}, use_global_device_ids=true | all-gather | bytes 196608 | tf_op jit(solution)/shard_map/all_gather | solution.py:50
  6.9 6.5 %all-to-all-start = ((s32[2,32,512]{2,0,1:T(2,128)}), s32[2,32,512]{2,0,1:T(2,128)S(1)}, u32[]{:S(2)}, u32[]{:S(2)}) async-start(s32[2,32,512]{2,0,1:T(2,128)} %all_gather.7), calls=%async_computation | async-start | bytes 262144 | tf_op jit(solution)/shard_map/all_to_all | solution.py:52
  13.4 0.0 copy-done
  13.4 3.2 %fusion.17 = bf16[16,1024]{1,0:T(8,128)(2,1)S(1)} fusion(bf16[16,1024]{1,0:T(8,128)(2,1)S(1)} %reshape.12), kind=kOutput, calls=%fused_computation.34 | convolution fusion | flops 55590912 | bytes 65536 | tf_op jit(solution)/shard_map/dot_general | solution.py:45
  16.7 23.3 %all_gather.6 = bf16[8,32,1024]{2,0,1:T(8,128)(2,1)S(1)} all-gather(bf16[8,2,1024]{2,0,1:T(8,128)(2,1)S(1)} %copy.8), channel_id=1, replica_groups=mesh['ang'=16,'sl'=2] {'ang'}, dimensions={1}, use_global_device_ids=true | all-gather | bytes 557056 | tf_op jit(solution)/shard_map/all_gather | solution.py:54
  39.9 0.0 all-to-all-done
  39.9 0.1 all_to_all.16
  40.0 37.5 %while.16 = (s32[]{:T(128)}, f32[2,8,512]{2,1,0:T(8,128)S(1)}, bf16[8,32,1024]{2,0,1:T(8,128)(2,1)S(1)}, s32[32,2,512]{2,0,1:T(8,128)S(1)}, s32[]{:T(128)}, /*index=5*/s32[]{:T(128)}, s32[]{:T(128)}, s32[]{:T(128)}) while((s32[]{:T(128)}, f32[2,8,512]{2,1,0:T(8,128)S(1)}, bf16[8,32,1024]{2,0,1:T(8,128)(2,1)S(1)}, ...), condition=%wide.region_1.2_spmd.clone, body=%wide.region_0.1_spmd.clone.sunk | while | flops 46215176 | bytes 180385 | solution.py:62
  40.1 2.3 %fusion.30 = f32[2,8,512]{2,1,0:T(8,128)S(1)} fusion(f32[2,2,512]{2,0,1:T(2,128)S(1)} %get-tuple-element.175, s32[2,2,512]{2,0,1:T(2,128)S(1)} %get-tuple-element.176, f32[2,2,512]{2,0,1:T(2,128)S(1)} %get-tuple-element.177, s32[2,2,512]{2,0,1:T(2,128)S(1)} %get-tuple-element.178, f32[2,8,512]{2,1,0:T(8,128)S(1)} %get-tuple-element.188, ...), kind=kOutput, calls=%fused_computation.5.clone.1 | convolution fusion | flops 46153728 | bytes 131077 | tf_op jit(solution)/shard_map/while/body/eval_jaxpr/arxb,sab->rsx/dot_general | solution.py:38
  42.5 2.3 %fusion.30 = f32[2,8,512]{2,1,0:T(8,128)S(1)} fusion(f32[2,2,512]{2,0,1:T(2,128)S(1)} %get-tuple-element.175, s32[2,2,512]{2,0,1:T(2,128)S(1)} %get-tuple-element.176, f32[2,2,512]{2,0,1:T(2,128)S(1)} %get-tuple-element.177, s32[2,2,512]{2,0,1:T(2,128)S(1)} %get-tuple-element.178, f32[2,8,512]{2,1,0:T(8,128)S(1)} %get-tuple-element.188, ...), kind=kOutput, calls=%fused_computation.5.clone.1 | convolution fusion | flops 46153728 | bytes 131077 | tf_op jit(solution)/shard_map/while/body/eval_jaxpr/arxb,sab->rsx/dot_general | solution.py:38
  44.8 2.3 %fusion.30 = f32[2,8,512]{2,1,0:T(8,128)S(1)} fusion(f32[2,2,512]{2,0,1:T(2,128)S(1)} %get-tuple-element.175, s32[2,2,512]{2,0,1:T(2,128)S(1)} %get-tuple-element.176, f32[2,2,512]{2,0,1:T(2,128)S(1)} %get-tuple-element.177, s32[2,2,512]{2,0,1:T(2,128)S(1)} %get-tuple-element.178, f32[2,8,512]{2,1,0:T(8,128)S(1)} %get-tuple-element.188, ...), kind=kOutput, calls=%fused_computation.5.clone.1 | convolution fusion | flops 46153728 | bytes 131077 | tf_op jit(solution)/shard_map/while/body/eval_jaxpr/arxb,sab->rsx/dot_general | solution.py:38
  47.2 2.3 %fusion.30 = f32[2,8,512]{2,1,0:T(8,128)S(1)} fusion(f32[2,2,512]{2,0,1:T(2,128)S(1)} %get-tuple-element.175, s32[2,2,512]{2,0,1:T(2,128)S(1)} %get-tuple-element.176, f32[2,2,512]{2,0,1:T(2,128)S(1)} %get-tuple-element.177, s32[2,2,512]{2,0,1:T(2,128)S(1)} %get-tuple-element.178, f32[2,8,512]{2,1,0:T(8,128)S(1)} %get-tuple-element.188, ...), kind=kOutput, calls=%fused_computation.5.clone.1 | convolution fusion | flops 46153728 | bytes 131077 | tf_op jit(solution)/shard_map/while/body/eval_jaxpr/arxb,sab->rsx/dot_general | solution.py:38
  49.5 2.3 %fusion.30 = f32[2,8,512]{2,1,0:T(8,128)S(1)} fusion(f32[2,2,512]{2,0,1:T(2,128)S(1)} %get-tuple-element.175, s32[2,2,512]{2,0,1:T(2,128)S(1)} %get-tuple-element.176, f32[2,2,512]{2,0,1:T(2,128)S(1)} %get-tuple-element.177, s32[2,2,512]{2,0,1:T(2,128)S(1)} %get-tuple-element.178, f32[2,8,512]{2,1,0:T(8,128)S(1)} %get-tuple-element.188, ...), kind=kOutput, calls=%fused_computation.5.clone.1 | convolution fusion | flops 46153728 | bytes 131077 | tf_op jit(solution)/shard_map/while/body/eval_jaxpr/arxb,sab->rsx/dot_general | solution.py:38
  51.9 2.3 %fusion.30 = f32[2,8,512]{2,1,0:T(8,128)S(1)} fusion(f32[2,2,512]{2,0,1:T(2,128)S(1)} %get-tuple-element.175, s32[2,2,512]{2,0,1:T(2,128)S(1)} %get-tuple-element.176, f32[2,2,512]{2,0,1:T(2,128)S(1)} %get-tuple-element.177, s32[2,2,512]{2,0,1:T(2,128)S(1)} %get-tuple-element.178, f32[2,8,512]{2,1,0:T(8,128)S(1)} %get-tuple-element.188, ...), kind=kOutput, calls=%fused_computation.5.clone.1 | convolution fusion | flops 46153728 | bytes 131077 | tf_op jit(solution)/shard_map/while/body/eval_jaxpr/arxb,sab->rsx/dot_general | solution.py:38
  54.2 2.3 %fusion.30 = f32[2,8,512]{2,1,0:T(8,128)S(1)} fusion(f32[2,2,512]{2,0,1:T(2,128)S(1)} %get-tuple-element.175, s32[2,2,512]{2,0,1:T(2,128)S(1)} %get-tuple-element.176, f32[2,2,512]{2,0,1:T(2,128)S(1)} %get-tuple-element.177, s32[2,2,512]{2,0,1:T(2,128)S(1)} %get-tuple-element.178, f32[2,8,512]{2,1,0:T(8,128)S(1)} %get-tuple-element.188, ...), kind=kOutput, calls=%fused_computation.5.clone.1 | convolution fusion | flops 46153728 | bytes 131077 | tf_op jit(solution)/shard_map/while/body/eval_jaxpr/arxb,sab->rsx/dot_general | solution.py:38
  56.5 2.3 %fusion.30 = f32[2,8,512]{2,1,0:T(8,128)S(1)} fusion(f32[2,2,512]{2,0,1:T(2,128)S(1)} %get-tuple-element.175, s32[2,2,512]{2,0,1:T(2,128)S(1)} %get-tuple-element.176, f32[2,2,512]{2,0,1:T(2,128)S(1)} %get-tuple-element.177, s32[2,2,512]{2,0,1:T(2,128)S(1)} %get-tuple-element.178, f32[2,8,512]{2,1,0:T(8,128)S(1)} %get-tuple-element.188, ...), kind=kOutput, calls=%fused_computation.5.clone.1 | convolution fusion | flops 46153728 | bytes 131077 | tf_op jit(solution)/shard_map/while/body/eval_jaxpr/arxb,sab->rsx/dot_general | solution.py:38
  58.9 2.3 %fusion.30 = f32[2,8,512]{2,1,0:T(8,128)S(1)} fusion(f32[2,2,512]{2,0,1:T(2,128)S(1)} %get-tuple-element.175, s32[2,2,512]{2,0,1:T(2,128)S(1)} %get-tuple-element.176, f32[2,2,512]{2,0,1:T(2,128)S(1)} %get-tuple-element.177, s32[2,2,512]{2,0,1:T(2,128)S(1)} %get-tuple-element.178, f32[2,8,512]{2,1,0:T(8,128)S(1)} %get-tuple-element.188, ...), kind=kOutput, calls=%fused_computation.5.clone.1 | convolution fusion | flops 46153728 | bytes 131077 | tf_op jit(solution)/shard_map/while/body/eval_jaxpr/arxb,sab->rsx/dot_general | solution.py:38
  61.2 2.3 %fusion.30 = f32[2,8,512]{2,1,0:T(8,128)S(1)} fusion(f32[2,2,512]{2,0,1:T(2,128)S(1)} %get-tuple-element.175, s32[2,2,512]{2,0,1:T(2,128)S(1)} %get-tuple-element.176, f32[2,2,512]{2,0,1:T(2,128)S(1)} %get-tuple-element.177, s32[2,2,512]{2,0,1:T(2,128)S(1)} %get-tuple-element.178, f32[2,8,512]{2,1,0:T(8,128)S(1)} %get-tuple-element.188, ...), kind=kOutput, calls=%fused_computation.5.clone.1 | convolution fusion | flops 46153728 | bytes 131077 | tf_op jit(solution)/shard_map/while/body/eval_jaxpr/arxb,sab->rsx/dot_general | solution.py:38
  63.6 2.3 %fusion.30 = f32[2,8,512]{2,1,0:T(8,128)S(1)} fusion(f32[2,2,512]{2,0,1:T(2,128)S(1)} %get-tuple-element.175, s32[2,2,512]{2,0,1:T(2,128)S(1)} %get-tuple-element.176, f32[2,2,512]{2,0,1:T(2,128)S(1)} %get-tuple-element.177, s32[2,2,512]{2,0,1:T(2,128)S(1)} %get-tuple-element.178, f32[2,8,512]{2,1,0:T(8,128)S(1)} %get-tuple-element.188, ...), kind=kOutput, calls=%fused_computation.5.clone.1 | convolution fusion | flops 46153728 | bytes 131077 | tf_op jit(solution)/shard_map/while/body/eval_jaxpr/arxb,sab->rsx/dot_general | solution.py:38
  65.9 2.3 %fusion.30 = f32[2,8,512]{2,1,0:T(8,128)S(1)} fusion(f32[2,2,512]{2,0,1:T(2,128)S(1)} %get-tuple-element.175, s32[2,2,512]{2,0,1:T(2,128)S(1)} %get-tuple-element.176, f32[2,2,512]{2,0,1:T(2,128)S(1)} %get-tuple-element.177, s32[2,2,512]{2,0,1:T(2,128)S(1)} %get-tuple-element.178, f32[2,8,512]{2,1,0:T(8,128)S(1)} %get-tuple-element.188, ...), kind=kOutput, calls=%fused_computation.5.clone.1 | convolution fusion | flops 46153728 | bytes 131077 | tf_op jit(solution)/shard_map/while/body/eval_jaxpr/arxb,sab->rsx/dot_general | solution.py:38
  68.3 2.3 %fusion.30 = f32[2,8,512]{2,1,0:T(8,128)S(1)} fusion(f32[2,2,512]{2,0,1:T(2,128)S(1)} %get-tuple-element.175, s32[2,2,512]{2,0,1:T(2,128)S(1)} %get-tuple-element.176, f32[2,2,512]{2,0,1:T(2,128)S(1)} %get-tuple-element.177, s32[2,2,512]{2,0,1:T(2,128)S(1)} %get-tuple-element.178, f32[2,8,512]{2,1,0:T(8,128)S(1)} %get-tuple-element.188, ...), kind=kOutput, calls=%fused_computation.5.clone.1 | convolution fusion | flops 46153728 | bytes 131077 | tf_op jit(solution)/shard_map/while/body/eval_jaxpr/arxb,sab->rsx/dot_general | solution.py:38
  70.6 2.3 %fusion.30 = f32[2,8,512]{2,1,0:T(8,128)S(1)} fusion(f32[2,2,512]{2,0,1:T(2,128)S(1)} %get-tuple-element.175, s32[2,2,512]{2,0,1:T(2,128)S(1)} %get-tuple-element.176, f32[2,2,512]{2,0,1:T(2,128)S(1)} %get-tuple-element.177, s32[2,2,512]{2,0,1:T(2,128)S(1)} %get-tuple-element.178, f32[2,8,512]{2,1,0:T(8,128)S(1)} %get-tuple-element.188, ...), kind=kOutput, calls=%fused_computation.5.clone.1 | convolution fusion | flops 46153728 | bytes 131077 | tf_op jit(solution)/shard_map/while/body/eval_jaxpr/arxb,sab->rsx/dot_general | solution.py:38
  72.9 2.3 %fusion.30 = f32[2,8,512]{2,1,0:T(8,128)S(1)} fusion(f32[2,2,512]{2,0,1:T(2,128)S(1)} %get-tuple-element.175, s32[2,2,512]{2,0,1:T(2,128)S(1)} %get-tuple-element.176, f32[2,2,512]{2,0,1:T(2,128)S(1)} %get-tuple-element.177, s32[2,2,512]{2,0,1:T(2,128)S(1)} %get-tuple-element.178, f32[2,8,512]{2,1,0:T(8,128)S(1)} %get-tuple-element.188, ...), kind=kOutput, calls=%fused_computation.5.clone.1 | convolution fusion | flops 46153728 | bytes 131077 | tf_op jit(solution)/shard_map/while/body/eval_jaxpr/arxb,sab->rsx/dot_general | solution.py:38
  75.3 2.3 %fusion.30 = f32[2,8,512]{2,1,0:T(8,128)S(1)} fusion(f32[2,2,512]{2,0,1:T(2,128)S(1)} %get-tuple-element.175, s32[2,2,512]{2,0,1:T(2,128)S(1)} %get-tuple-element.176, f32[2,2,512]{2,0,1:T(2,128)S(1)} %get-tuple-element.177, s32[2,2,512]{2,0,1:T(2,128)S(1)} %get-tuple-element.178, f32[2,8,512]{2,1,0:T(8,128)S(1)} %get-tuple-element.188, ...), kind=kOutput, calls=%fused_computation.5.clone.1 | convolution fusion | flops 46153728 | bytes 131077 | tf_op jit(solution)/shard_map/while/body/eval_jaxpr/arxb,sab->rsx/dot_general | solution.py:38
  77.6 0.6 broadcast_multiply_fusion
  (37 shorter events, 1.1 us)
Async XLA Ops:
  0.0 13.4 %copy-start = (bf16[8,2,1024]{2,1,0:T(2,128)(2,1)S(1)}, bf16[8,2,1024]{2,1,0:T(2,128)(2,1)}, u32[]{:S(2)}) copy-start(bf16[8,2,1024]{2,1,0:T(2,128)(2,1)} %param.4) | copy-start | bytes 98308
  6.9 33.0 %all-to-all-start = ((s32[2,32,512]{2,0,1:T(2,128)}), s32[2,32,512]{2,0,1:T(2,128)S(1)}, u32[]{:S(2)}, u32[]{:S(2)}) async-start(s32[2,32,512]{2,0,1:T(2,128)} %all_gather.7), calls=%async_computation | async-start | bytes 262144 | tf_op jit(solution)/shard_map/all_to_all | solution.py:52
where the time goes:
time: 78.4 us; the launch traced here: 78.2 us
  matrix products  39.4 us (50%)
  blocking collectives  29.2 us (37%)
  starting transfers between devices  6.49 us (8%)
  other arithmetic  1.68 us (2%)
  local copies, waits for them, and re-layouts  1.06 us (1%)
    dot_general x16, matrix products, project_block(): jnp.einsum('arxb,sab->rsx', weights, projections, preferred_element_type=...  36.2 us
    all_gather x1, blocking collectives, shards(): shard_piece = lax.all_gather(filtered, 'ang', axis=1, tiled=True)  23.3 us
    all_to_all x1, starting transfers between devices, shards(): lax.all_to_all(coord_table, 'ang', split_axis=1, concat_axis=0, tiled=True)  6.49 us
    all_gather x1, blocking collectives, shards(): coord_table = lax.all_gather(detector_coord, 'sl', axis=1, tiled=True)  5.97 us
    dot_general x1, matrix products, shards(): jnp.dot(sinogram.reshape(slices * angles, bin_count), table, preferred_el...  3.19 us
  transfers between devices with their start and end apart: 1, of which 0 were waited for; matrix products, arithmetic and copies ran while one was open for 4% of the time, Pallas kernels for 0%

commit v1 on v0

v1 whole, which is shorter than its diff:
```python
import functools
import math

import jax
import jax.numpy as jnp
from jax import lax
from jax.experimental import pallas as pl
from jax.experimental.pallas import tpu as pltpu
from jax.sharding import PartitionSpec as P

LANES = 128
FRACTION_BITS = 20


def ramp_block(size, shift):
    first = lax.broadcasted_iota(jnp.int32, (size, size), 0)
    second = lax.broadcasted_iota(jnp.int32, (size, size), 1)
    offset = second - first + shift
    offset_sq = jnp.maximum((offset * offset).astype(jnp.float32), jnp.float32(1.0))
    values = jnp.where(
        offset == 0,
        jnp.float32(0.25),
        jnp.where(
            (offset & 1) != 0, jnp.float32(-1.0 / math.pi**2) / offset_sq, jnp.float32(0.0)
        ),
    )
    return values.astype(jnp.bfloat16)


def build_ramp(ramp, size, count):
    for step in range(2 * count - 1):
        ramp[step] = ramp_block(size, (step - count + 1) * size)


def filter_rows(sino, ramp, tiles, size, count):
    rows = sino.shape[0]
    per_row = sino.shape[1] // LANES
    for out_block in range(count):
        total = None
        for in_block in range(count):
            part = jnp.dot(
                sino[:, in_block * size : (in_block + 1) * size],
                ramp[out_block - in_block + count - 1],
                preferred_element_type=jnp.float32,
            )
            total = part if total is None else total + part
        total = total.astype(jnp.bfloat16).astype(jnp.float32)
        for piece in range(size // LANES):
            h = out_block * (size // LANES) + piece
            tiles[pl.ds(h, rows, stride=per_row), :] = total[:, piece * LANES : (piece + 1) * LANES]


def pick(tile, index):
    return jnp.take_along_axis(tile, index, axis=1, mode="promise_in_bounds")


def interpolate(coords, tiles, out, scale, angles, slices, per_row, together=2):
    rows, width = coords.shape[-2], coords.shape[-1]
    level = lax.broadcasted_iota(jnp.int32, (per_row, LANES), 0)
    spots = [(r, x) for r in range(rows) for x in range(width // LANES)]
    for start in range(0, len(spots), together):
        group = spots[start : start + together]

        def one_angle(a, sums):
            picks = []
            for r, x in group:
                c = coords[a, pl.ds(r, 1), pl.ds(x * LANES, LANES)]
                c = jnp.broadcast_to(c, (per_row, LANES))
                left = c >> FRACTION_BITS
                right = left + 1
                fraction = (c & (2**FRACTION_BITS - 1)).astype(jnp.float32) * jnp.float32(
                    2.0**-FRACTION_BITS
                )
                w_left = (1.0 - fraction).astype(jnp.bfloat16).astype(jnp.float32)
                w_right = fraction.astype(jnp.bfloat16).astype(jnp.float32)
                w_left = jnp.where(left >> 7 == level, w_left, 0.0)
                w_right = jnp.where(right >> 7 == level, w_right, 0.0)
                picks.append((left & (LANES - 1), right & (LANES - 1), w_left, w_right))
            new = []
            for s in range(slices):
                row = pl.multiple_of((s * angles + a) * per_row, per_row)
                tile = tiles[pl.ds(row, per_row), :]
                for g, (i_left, i_right, w_left, w_right) in enumerate(picks):
                    term = w_left * pick(tile, i_left) + w_right * pick(tile, i_right)
                    new.append(sums[s * len(group) + g] + term)
            return tuple(new)

        zero = jnp.zeros((per_row, LANES), jnp.float32)
        sums = lax.fori_loop(0, angles, one_angle, (zero,) * (slices * len(group)), unroll=2)
        for s in range(slices):
            for g, (r, x) in enumerate(group):
                line = jnp.sum(sums[s * len(group) + g], axis=0, keepdims=True) * scale
                out[r, pl.ds(s, 1), pl.ds(x * LANES, LANES)] = line


def kernel(angles, slices, sino, coords, out, ramp, tiles):
    bins = sino.shape[1]
    size = ramp.shape[1]
    build_ramp(ramp, size, bins // size)
    filter_rows(sino, ramp, tiles, size, bins // size)
    scale = jnp.float32(math.pi / angles)
    interpolate(coords, tiles, out, scale, angles, slices, bins // LANES)


def shards(sinogram, detector_coord):
    slices, own_angles, bins = sinogram.shape
    width = detector_coord.shape[2]
    groups = lax.axis_size("ang")
    angles = own_angles * groups
    coord_table = lax.all_gather(detector_coord, "sl", axis=1, tiled=True)
    row_share = coord_table.shape[1] // groups
    own_rows = lax.all_to_all(coord_table, "ang", split_axis=1, concat_axis=0, tiled=True)
    sino = lax.all_gather(sinogram, "ang", axis=1, tiled=True).reshape(slices * angles, bins)
    size = 256
    return pl.pallas_call(
        functools.partial(kernel, angles, slices),
        out_shape=jax.ShapeDtypeStruct((row_share, slices, width), jnp.float32),
        in_specs=[pl.BlockSpec(memory_space=pltpu.VMEM)] * 2,
        out_specs=pl.BlockSpec(memory_space=pltpu.VMEM),
        scratch_shapes=[
            pltpu.VMEM((2 * (bins // size) - 1, size, size), jnp.bfloat16),
            pltpu.VMEM((slices * angles * bins // LANES, LANES), jnp.float32),
        ],
    )(sino, own_rows)


def solution(mesh):
    in_specs = (P("sl", "ang", None), P("ang", "sl", None))
    out_specs = P("ang", "sl", None)
    return jax.shard_map(shards, mesh=mesh, in_specs=in_specs, out_specs=out_specs, check_vma=False)
```

time: 78.4 us -> 57.6 us (0.73)
  matrix products: 39.4 us -> 0 us
  Pallas kernels: 0 us -> 18.8 us
  other arithmetic: 1.68 us -> 0 us
  local copies, waits for them, and re-layouts: 1.06 us -> 2.7 us
    dot_general x17 -> x0, matrix products: 39.4 us -> none  [the longest x16 36.2 us: project_block(): jnp.einsum('arxb,sab->rsx', weights, projections, preferred_element_type=...]
    pallas_call x0 -> x1, Pallas kernels: none -> 18.8 us  [shards(): pl.pallas_call(functools.partial(kernel, angles, slices), out_shape=jax.S...]
    all_gather x0 -> x1, local copies, waits for them, and re-layouts: none -> 1.08 us  [shards(): lax.all_gather(sinogram, 'ang', axis=1, tiled=True)]
  transfers between devices with their start and end apart: 1 -> 1, of which waited for: 0 -> 0; matrix products, arithmetic and copies ran while one was open for 4% -> 2% of each run, Pallas kernels for 0% -> 0%
where the time goes in v1:
time: 57.6 us; the launch traced here: 57.3 us
  blocking collectives  29.1 us (51%)
  Pallas kernels  18.8 us (33%)
  starting transfers between devices  6.62 us (11%)
  local copies, waits for them, and re-layouts  2.7 us (5%)
    all_gather x1, blocking collectives, shards(): lax.all_gather(sinogram, 'ang', axis=1, tiled=True)  23.2 us
    pallas_call x1, Pallas kernels, shards(): pl.pallas_call(functools.partial(kernel, angles, slices), out_shape=jax.S...  18.8 us
    all_to_all x1, starting transfers between devices, shards(): lax.all_to_all(coord_table, 'ang', split_axis=1, concat_axis=0, tiled=True)  6.62 us
    all_gather x1, blocking collectives, shards(): coord_table = lax.all_gather(detector_coord, 'sl', axis=1, tiled=True)  5.97 us
  transfers between devices with their start and end apart: 1, of which 0 were waited for; matrix products, arithmetic and copies ran while one was open for 2% of the time, Pallas kernels for 0%

profile of v1, /device:TPU:0, one launch (start us, length us, event | category | flops | bytes accessed | tf_op | source)
XLA Modules:
  0.0 57.3 jit_solution(449618165834328915)
XLA Ops:
  0.0 0.9 %copy.10 = s32[2,16,512]{2,0,1:T(2,128)S(1)} copy(s32[2,16,512]{2,1,0:T(8,128)} %param.3) | data formatting | bytes 131072 | tf_op args[1]
  0.9 6.0 %all_gather.7 = s32[2,32,512]{2,0,1:T(2,128)} all-gather(s32[2,16,512]{2,0,1:T(2,128)S(1)} %copy.10), channel_id=1, replica_groups=mesh['ang'=16,'sl'=2] {'sl'}, dimensions={1}, use_global_device_ids=true | all-gather | bytes 196608 | tf_op jit(solution)/shard_map/all_gather | solution.py:110
  6.9 0.0 copy-start
  6.9 6.6 %all-to-all-start = ((s32[2,32,512]{2,0,1:T(2,128)}), s32[2,32,512]{2,0,1:T(2,128)S(1)}, u32[]{:S(2)}, u32[]{:S(2)}) async-start(s32[2,32,512]{2,0,1:T(2,128)} %all_gather.7), calls=%async_computation | async-start | bytes 262144 | tf_op jit(solution)/shard_map/all_to_all | solution.py:112
  13.5 0.0 copy-done
  13.5 23.2 %all_gather.6 = bf16[8,32,1024]{2,0,1:T(8,128)(2,1)S(1)} all-gather(bf16[8,2,1024]{2,0,1:T(8,128)(2,1)S(1)} %copy.8), channel_id=1, replica_groups=mesh['ang'=16,'sl'=2] {'ang'}, dimensions={1}, use_global_device_ids=true | all-gather | bytes 557056 | tf_op jit(solution)/shard_map/all_gather | solution.py:113
  36.7 1.1 %copy.9 = bf16[8,32,1024]{2,1,0:T(8,128)(2,1)} copy(bf16[8,32,1024]{2,0,1:T(8,128)(2,1)S(1)} %all_gather.6) | data formatting | bytes 1048576 | tf_op jit(solution)/shard_map/all_gather | solution.py:113
  37.8 0.0 all-to-all-done
  37.8 0.7 %copy.11 = s32[2,16,2,512]{3,2,0,1:T(2,128)} copy(s32[2,16,2,512]{3,0,2,1:T(2,128)S(1)} %bitcast.6) | data formatting | bytes 262144 | tf_op jit(solution)/shard_map/all_to_all | solution.py:112
  38.5 18.8 %shard_map.28 = f32[2,8,512]{2,1,0:T(8,128)} custom-call(bf16[256,1024]{1,0:T(8,128)(2,1)} %bitcast.5, s32[32,2,512]{2,1,0:T(2,128)} %bitcast.7), custom_call_target="tpu_custom_call" | custom-call | tf_op jit(solution)/shard_map/pallas_call | solution.py:115
  (1 shorter events, 0.0 us)
Async XLA Ops:
  6.9 6.6 %copy-start = (bf16[8,2,1024]{2,1,0:T(2,128)(2,1)S(1)}, bf16[8,2,1024]{2,1,0:T(2,128)(2,1)}, u32[]{:S(2)}) copy-start(bf16[8,2,1024]{2,1,0:T(2,128)(2,1)} %param.2) | copy-start | bytes 98308
  6.9 30.9 %all-to-all-start = ((s32[2,32,512]{2,0,1:T(2,128)}), s32[2,32,512]{2,0,1:T(2,128)S(1)}, u32[]{:S(2)}, u32[]{:S(2)}) async-start(s32[2,32,512]{2,0,1:T(2,128)} %all_gather.7), calls=%async_computation | async-start | bytes 262144 | tf_op jit(solution)/shard_map/all_to_all | solution.py:112

commit v2 on v1

v2 whole, which is shorter than its diff:
```python
import functools
import math

import jax
import jax.numpy as jnp
from jax import lax
from jax.experimental import pallas as pl
from jax.experimental.pallas import tpu as pltpu
from jax.sharding import PartitionSpec as P

LANES = 128
FRACTION_BITS = 20


def ramp_block(size, shift):
    first = lax.broadcasted_iota(jnp.int32, (size, size), 0)
    second = lax.broadcasted_iota(jnp.int32, (size, size), 1)
    offset = second - first + shift
    offset_sq = jnp.maximum((offset * offset).astype(jnp.float32), jnp.float32(1.0))
    values = jnp.where(
        offset == 0,
        jnp.float32(0.25),
        jnp.where(
            (offset & 1) != 0, jnp.float32(-1.0 / math.pi**2) / offset_sq, jnp.float32(0.0)
        ),
    )
    return values.astype(jnp.bfloat16)


def build_ramp(ramp, size, count):
    for step in range(2 * count - 1):
        ramp[step] = ramp_block(size, (step - count + 1) * size)


def filter_rows(sino, ramp, tiles, size, count):
    rows = sino.shape[0]
    per_row = sino.shape[1] // LANES
    for out_block in range(count):
        total = None
        for in_block in range(count):
            part = jnp.dot(
                sino[:, in_block * size : (in_block + 1) * size],
                ramp[out_block - in_block + count - 1],
                preferred_element_type=jnp.float32,
            )
            total = part if total is None else total + part
        total = total.astype(jnp.bfloat16).astype(jnp.float32)
        for piece in range(size // LANES):
            h = out_block * (size // LANES) + piece
            tiles[pl.ds(h, rows, stride=per_row), :] = total[:, piece * LANES : (piece + 1) * LANES]


def pick(tile, index):
    return jnp.take_along_axis(tile, index, axis=1, mode="promise_in_bounds")


def interpolate(coords, tiles, out, scale, own_angles, together=2):
    rows, slices, width = out.shape
    groups = coords.shape[0]
    per_row = tiles.shape[0] // (groups * slices * own_angles)
    across = width // LANES
    level = lax.broadcasted_iota(jnp.int32, (per_row, LANES), 0)
    spots = [(r, x) for r in range(rows) for x in range(across)]
    for start in range(0, len(spots), together):
        group = spots[start : start + together]

        def one_group(g, sums):
            sums = list(sums)
            for al in range(own_angles):
                picks = []
                for r, x in group:
                    c = coords[g, pl.ds((al * rows + r) * across + x, 1), :]
                    c = jnp.broadcast_to(c, (per_row, LANES))
                    left = c >> FRACTION_BITS
                    right = left + 1
                    fraction = (c & (2**FRACTION_BITS - 1)).astype(jnp.float32) * jnp.float32(
                        2.0**-FRACTION_BITS
                    )
                    w_left = (1.0 - fraction).astype(jnp.bfloat16).astype(jnp.float32)
                    w_right = fraction.astype(jnp.bfloat16).astype(jnp.float32)
                    w_left = jnp.where(left >> 7 == level, w_left, 0.0)
                    w_right = jnp.where(right >> 7 == level, w_right, 0.0)
                    picks.append((left & (LANES - 1), right & (LANES - 1), w_left, w_right))
                for s in range(slices):
                    row = ((g * slices + s) * own_angles + al) * per_row
                    tile = tiles[pl.ds(pl.multiple_of(row, per_row), per_row), :]
                    for i, (i_left, i_right, w_left, w_right) in enumerate(picks):
                        term = w_left * pick(tile, i_left) + w_right * pick(tile, i_right)
                        sums[s * len(group) + i] = sums[s * len(group) + i] + term
            return tuple(sums)

        zero = jnp.zeros((per_row, LANES), jnp.float32)
        sums = lax.fori_loop(0, groups, one_group, (zero,) * (slices * len(group)))
        for s in range(slices):
            for i, (r, x) in enumerate(group):
                line = jnp.sum(sums[s * len(group) + i], axis=0, keepdims=True) * scale
                out[r, pl.ds(s, 1), pl.ds(x * LANES, LANES)] = line


def project_kernel(own_angles, sino, coords, out, ramp, tiles):
    bins = sino.shape[1]
    size = ramp.shape[1]
    build_ramp(ramp, size, bins // size)
    filter_rows(sino, ramp, tiles, size, bins // size)
    scale = jnp.float32(math.pi / (own_angles * coords.shape[0]))
    interpolate(coords, tiles, out, scale, own_angles)


def exchange_kernel(
    groups, halves, sino, coords, all_sino, all_coords,
    local_sem, s_send, s_recv, f_send, c_send, c_recv,
):
    me, half = lax.axis_index("ang"), lax.axis_index("sl")
    chip, core = me // 2, me % 2
    chips = groups // 2
    mate = chip * 2 + 1 - core
    total = groups * halves
    share = coords.shape[0]

    barrier = pltpu.get_barrier_semaphore()

    def greet(k, carry):
        there = lax.rem(me * halves + half + k, total)
        pl.semaphore_signal(
            barrier, inc=1, device_id={"ang": there // halves, "sl": there % halves},
            device_id_type=pl.DeviceIdType.MESH,
        )
        return carry

    lax.fori_loop(1, total, greet, 0)
    own = pltpu.make_async_copy(sino, all_sino.at[me], local_sem.at[0])
    own.start()
    pl.semaphore_wait(barrier, total - 1)

    def sino_copy(source, block, target, send_sem):
        return pltpu.make_async_remote_copy(
            src_ref=source, dst_ref=all_sino.at[block], send_sem=send_sem,
            recv_sem=s_recv.at[block], device_id={"ang": target},
            device_id_type=pl.DeviceIdType.MESH,
        )

    for k in range(chips - 1, 0, -1):
        sino_copy(sino, me, lax.rem(chip + k, chips) * 2 + core, s_send.at[k]).start()
    sino_copy(sino, me, mate, f_send.at[0]).start()

    def coord_copy(j, t):
        place = lax.rem(me + j, share)
        side = lax.rem(half + t, halves)
        target = half * share + place
        return target, side, coords.at[place], c_send.at[j * halves + t]

    def coord_remote(j, t):
        target, side, block, sem = coord_copy(j, t)
        return pltpu.make_async_remote_copy(
            src_ref=block, dst_ref=all_coords.at[me], send_sem=sem,
            recv_sem=c_recv.at[me], device_id={"ang": target, "sl": side},
            device_id_type=pl.DeviceIdType.MESH,
        )

    source_half = me // share
    at_home = source_half == half
    for j in range(share):
        for t in range(halves):
            if j == 0 and t == 0:
                @pl.when(at_home)
                def _():
                    pltpu.make_async_copy(
                        coords.at[lax.rem(me, share)], all_coords.at[me], c_recv.at[me]
                    ).start()

                @pl.when(jnp.logical_not(at_home))
                def _():
                    coord_remote(0, 0).start()
            else:
                coord_remote(j, t).start()

    for k in range(1, chips):
        block = lax.rem(chip + k, chips) * 2 + core
        sino_copy(sino, block, mate, f_send.at[k]).wait_recv()
        sino_copy(all_sino.at[block], block, mate, f_send.at[k]).start()
    for k in range(chips):
        block = lax.rem(chip + k, chips) * 2 + 1 - core
        sino_copy(sino, block, mate, f_send.at[0]).wait_recv()
    for g in range(groups):
        pltpu.make_async_copy(coords.at[0], all_coords.at[g], c_recv.at[g]).wait()
    own.wait()
    for k in range(1, chips):
        sino_copy(sino, me, mate, s_send.at[k]).wait_send()
    for k in range(chips):
        sino_copy(sino, me, mate, f_send.at[k]).wait_send()
    for j in range(share):
        for t in range(halves):
            if j == 0 and t == 0:
                @pl.when(jnp.logical_not(at_home))
                def _():
                    coord_remote(0, 0).wait_send()
            else:
                coord_remote(j, t).wait_send()


def shards(sinogram, detector_coord):
    slices, own_angles, bins = sinogram.shape
    local_rows, width = detector_coord.shape[1:]
    groups, halves = lax.axis_size("ang"), lax.axis_size("sl")
    row_share = local_rows * halves // groups
    share = local_rows // row_share
    sino = sinogram.reshape(slices * own_angles, bins)
    coords = detector_coord.reshape(own_angles, share, row_share, width)
    coords = coords.transpose(1, 0, 2, 3).reshape(share, -1, LANES)
    vmem = pl.BlockSpec(memory_space=pltpu.VMEM)
    all_sino, all_coords = pl.pallas_call(
        functools.partial(exchange_kernel, groups, halves),
        out_shape=(
            jax.ShapeDtypeStruct((groups,) + sino.shape, sino.dtype),
            jax.ShapeDtypeStruct((groups,) + coords.shape[1:], coords.dtype),
        ),
        in_specs=[vmem] * 2,
        out_specs=(vmem, vmem),
        scratch_shapes=[
            pltpu.SemaphoreType.DMA((1,)),
            pltpu.SemaphoreType.DMA((groups // 2,)),
            pltpu.SemaphoreType.DMA((groups,)),
            pltpu.SemaphoreType.DMA((groups // 2,)),
            pltpu.SemaphoreType.DMA((groups,)),
            pltpu.SemaphoreType.DMA((groups,)),
        ],
        compiler_params=pltpu.CompilerParams(collective_id=0, has_side_effects=True),
    )(sino, coords)
    size = 256
    return pl.pallas_call(
        functools.partial(project_kernel, own_angles),
        out_shape=jax.ShapeDtypeStruct((row_share, slices, width), jnp.float32),
        in_specs=[vmem] * 2,
        out_specs=vmem,
        scratch_shapes=[
            pltpu.VMEM((2 * (bins // size) - 1, size, size), jnp.bfloat16),
            pltpu.VMEM((groups * slices * own_angles * bins // LANES, LANES), jnp.float32),
        ],
    )(all_sino.reshape(groups * slices * own_angles, bins), all_coords)


def solution(mesh):
    in_specs = (P("sl", "ang", None), P("ang", "sl", None))
    out_specs = P("ang", "sl", None)
    return jax.shard_map(shards, mesh=mesh, in_specs=in_specs, out_specs=out_specs, check_vma=False)
```

time: 57.6 us -> 43.2 us (0.75)
  blocking collectives: 29.1 us -> 0 us
  Pallas kernels: 18.8 us -> 40.8 us
  starting transfers between devices: 6.62 us -> 0 us
    all_gather x2 -> x0, blocking collectives: 29.1 us -> none  [the longest x1 23.2 us: shards(): lax.all_gather(sinogram, 'ang', axis=1, tiled=True)]
    pallas_call x1 -> x2, Pallas kernels: 18.8 us -> 40.8 us  [the longest x1 22 us: shards(): pl.pallas_call(functools.partial(exchange_kernel, groups, halves), out_sh...]
    all_to_all x1 -> x0, starting transfers between devices: 6.62 us -> none  [shards(): lax.all_to_all(coord_table, 'ang', split_axis=1, concat_axis=0, tiled=True)]
    reshape x0 -> x4, local copies, waits for them, and re-layouts: none -> 2.14 us  [the longest x1 1.42 us: shards(): sino = sinogram.reshape(slices * own_angles, bins)]
    all_gather x1 -> x0, local copies, waits for them, and re-layouts: 1.08 us -> none  [shards(): lax.all_gather(sinogram, 'ang', axis=1, tiled=True)]
    unnamed x4 -> x2, local copies, waits for them, and re-layouts: 0.9 us -> 0.01 us
    all_to_all x1 -> x0, local copies, waits for them, and re-layouts: 0.71 us -> none  [shards(): lax.all_to_all(coord_table, 'ang', split_axis=1, concat_axis=0, tiled=True)]
  transfers between devices with their start and end apart: 1 -> 0, of which waited for: 0 -> 0; matrix products, arithmetic and copies ran while one was open for 2% -> 0% of each run, Pallas kernels for 0% -> 0%
where the time goes in v2:
time: 43.2 us; the launch traced here: 43 us
  Pallas kernels  40.8 us (94%)
  local copies, waits for them, and re-layouts  2.15 us (5%)
    pallas_call x1, Pallas kernels, shards(): pl.pallas_call(functools.partial(exchange_kernel, groups, halves), out_sh...  22 us
    pallas_call x1, Pallas kernels, shards(): pl.pallas_call(functools.partial(project_kernel, own_angles), out_shape=j...  18.8 us
    reshape x1, local copies, waits for them, and re-layouts, shards(): sino = sinogram.reshape(slices * own_angles, bins)  1.42 us

profile of v2, /device:TPU:0, one launch (start us, length us, event | category | flops | bytes accessed | tf_op | source)
XLA Modules:
  0.0 43.0 jit_solution(14605649106902539050)
XLA Ops:
  0.0 0.0 copy-start
  0.0 1.4 %reshape.12.sino = bf16[16,1024]{1,0:T(8,128)(2,1)} reshape(bf16[8,2,1024]{2,1,0:T(2,128)(2,1)} %param.2) | data formatting | bytes 65536 | tf_op jit(solution)/shard_map/reshape | solution.py:207
  1.4 0.0 copy-done
  1.5 0.7 %reshape.14.coords = s32[8,16,128]{2,1,0:T(8,128)} reshape(s32[8,2,2,512]{3,2,1,0:T(2,128)S(1)} %bitcast.5) | data formatting | bytes 131072 | tf_op jit(solution)/shard_map/reshape | solution.py:209
  2.2 22.0 %shard_map.28 = (bf16[16,16,1024]{2,1,0:T(8,128)(2,1)}, s32[16,16,128]{2,1,0:T(8,128)}) custom-call(bf16[16,1024]{1,0:T(8,128)(2,1)} %reshape.12.sino, s32[8,16,128]{2,1,0:T(8,128)} %reshape.14.coords), custom_call_target="tpu_custom_call" | custom-call | tf_op jit(solution)/shard_map/pallas_call | solution.py:211
  24.2 18.8 %shard_map.29 = f32[2,8,512]{2,1,0:T(8,128)} custom-call(bf16[256,1024]{1,0:T(8,128)(2,1)} %bitcast.4, s32[16,16,128]{2,1,0:T(8,128)} %get-tuple-element.8.coords), custom_call_target="tpu_custom_call" | custom-call | tf_op jit(solution)/shard_map/pallas_call | solution.py:230
  (2 shorter events, 0.0 us)
Async XLA Ops:
  0.0 1.4 %copy-start = (s32[2,16,512]{2,1,0:T(8,128)S(1)}, s32[2,16,512]{2,1,0:T(8,128)}, u32[]{:S(2)}) copy-start(s32[2,16,512]{2,1,0:T(8,128)} %param.3) | copy-start | bytes 196612

commit v3 on v2

--- a/solution.py
+++ b/solution.py
@@ -81,12 +81,15 @@
                     w_left = jnp.where(left >> 7 == level, w_left, 0.0)
                     w_right = jnp.where(right >> 7 == level, w_right, 0.0)
                     picks.append((left & (LANES - 1), right & (LANES - 1), w_left, w_right))
+                held = []
                 for s in range(slices):
                     row = ((g * slices + s) * own_angles + al) * per_row
-                    tile = tiles[pl.ds(pl.multiple_of(row, per_row), per_row), :]
-                    for i, (i_left, i_right, w_left, w_right) in enumerate(picks):
-                        term = w_left * pick(tile, i_left) + w_right * pick(tile, i_right)
-                        sums[s * len(group) + i] = sums[s * len(group) + i] + term
+                    held.append(tiles[pl.ds(pl.multiple_of(row, per_row), per_row), :])
+                for i, (i_left, i_right, w_left, w_right) in enumerate(picks):
+                    for index, weight in ((i_left, w_left), (i_right, w_right)):
+                        for s in range(slices):
+                            at = s * len(group) + i
+                            sums[at] = sums[at] + weight * pick(held[s], index)
             return tuple(sums)
 
         zero = jnp.zeros((per_row, LANES), jnp.float32)

time: 43.2 us -> 37.7 us (0.87)
  Pallas kernels: 40.8 us -> 35.4 us
    pallas_call x1, Pallas kernels: 18.8 us -> 13.3 us  [shards(): pl.pallas_call(functools.partial(project_kernel, own_angles), out_shape=j...]
where the time goes in v3:
time: 37.7 us; the launch traced here: 37.5 us
  Pallas kernels  35.4 us (94%)
  local copies, waits for them, and re-layouts  2.15 us (6%)
    pallas_call x1, Pallas kernels, shards(): pl.pallas_call(functools.partial(exchange_kernel, groups, halves), out_sh...  22 us
    pallas_call x1, Pallas kernels, shards(): pl.pallas_call(functools.partial(project_kernel, own_angles), out_shape=j...  13.3 us
    reshape x1, local copies, waits for them, and re-layouts, shards(): sino = sinogram.reshape(slices * own_angles, bins)  1.42 us

profile of v3, /device:TPU:0, one launch (start us, length us, event | category | flops | bytes accessed | tf_op | source)
XLA Modules:
  0.0 37.5 jit_solution(9805906370601233428)
XLA Ops:
  0.0 0.0 copy-start
  0.0 1.4 %reshape.12.sino = bf16[16,1024]{1,0:T(8,128)(2,1)} reshape(bf16[8,2,1024]{2,1,0:T(2,128)(2,1)} %param.2) | data formatting | bytes 65536 | tf_op jit(solution)/shard_map/reshape | solution.py:210
  1.4 0.0 copy-done
  1.5 0.7 %reshape.14.coords = s32[8,16,128]{2,1,0:T(8,128)} reshape(s32[8,2,2,512]{3,2,1,0:T(2,128)S(1)} %bitcast.5) | data formatting | bytes 131072 | tf_op jit(solution)/shard_map/reshape | solution.py:212
  2.2 22.0 %shard_map.28 = (bf16[16,16,1024]{2,1,0:T(8,128)(2,1)}, s32[16,16,128]{2,1,0:T(8,128)}) custom-call(bf16[16,1024]{1,0:T(8,128)(2,1)} %reshape.12.sino, s32[8,16,128]{2,1,0:T(8,128)} %reshape.14.coords), custom_call_target="tpu_custom_call" | custom-call | tf_op jit(solution)/shard_map/pallas_call | solution.py:214
  24.2 13.3 %shard_map.29 = f32[2,8,512]{2,1,0:T(8,128)} custom-call(bf16[256,1024]{1,0:T(8,128)(2,1)} %bitcast.4, s32[16,16,128]{2,1,0:T(8,128)} %get-tuple-element.8.coords), custom_call_target="tpu_custom_call" | custom-call | tf_op jit(solution)/shard_map/pallas_call | solution.py:233
  (2 shorter events, 0.0 us)
Async XLA Ops:
  0.0 1.4 %copy-start = (s32[2,16,512]{2,1,0:T(8,128)S(1)}, s32[2,16,512]{2,1,0:T(8,128)}, u32[]{:S(2)}) copy-start(s32[2,16,512]{2,1,0:T(8,128)} %param.3) | copy-start | bytes 196612

commit v4 on v3

--- a/solution.py
+++ b/solution.py
@@ -111,12 +111,12 @@
 
 def exchange_kernel(
     groups, halves, sino, coords, all_sino, all_coords,
-    local_sem, s_send, s_recv, f_send, c_send, c_recv,
+    local_sem, s_send, n_send, f_send, s_recv, c_send, x_send, c_recv,
 ):
     me, half = lax.axis_index("ang"), lax.axis_index("sl")
-    chip, core = me // 2, me % 2
-    chips = groups // 2
-    mate = chip * 2 + 1 - core
+    outer, outers = me // 4, groups // 4
+    mate = me + 1 - 2 * (me % 2)
+    near = me + 2 - 4 * (me // 2 % 2)
     total = groups * halves
     share = coords.shape[0]
 
@@ -135,70 +135,89 @@
     own.start()
     pl.semaphore_wait(barrier, total - 1)
 
-    def sino_copy(source, block, target, send_sem):
+    def sino_copy(block, target, send_sem, source=None):
         return pltpu.make_async_remote_copy(
-            src_ref=source, dst_ref=all_sino.at[block], send_sem=send_sem,
+            src_ref=all_sino.at[block] if source is None else source,
+            dst_ref=all_sino.at[block], send_sem=send_sem,
             recv_sem=s_recv.at[block], device_id={"ang": target},
             device_id_type=pl.DeviceIdType.MESH,
         )
 
-    for k in range(chips - 1, 0, -1):
-        sino_copy(sino, me, lax.rem(chip + k, chips) * 2 + core, s_send.at[k]).start()
-    sino_copy(sino, me, mate, f_send.at[0]).start()
-
-    def coord_copy(j, t):
-        place = lax.rem(me + j, share)
-        side = lax.rem(half + t, halves)
-        target = half * share + place
-        return target, side, coords.at[place], c_send.at[j * halves + t]
-
-    def coord_remote(j, t):
-        target, side, block, sem = coord_copy(j, t)
+    def coord_copy(block, target, side, send_sem, source=None):
         return pltpu.make_async_remote_copy(
-            src_ref=block, dst_ref=all_coords.at[me], send_sem=sem,
-            recv_sem=c_recv.at[me], device_id={"ang": target, "sl": side},
+            src_ref=all_coords.at[block] if source is None else source,
+            dst_ref=all_coords.at[block], send_sem=send_sem,
+            recv_sem=c_recv.at[block], device_id={"ang": target, "sl": side},
             device_id_type=pl.DeviceIdType.MESH,
         )
 
-    source_half = me // share
-    at_home = source_half == half
-    for j in range(share):
-        for t in range(halves):
-            if j == 0 and t == 0:
-                @pl.when(at_home)
-                def _():
-                    pltpu.make_async_copy(
-                        coords.at[lax.rem(me, share)], all_coords.at[me], c_recv.at[me]
-                    ).start()
-
-                @pl.when(jnp.logical_not(at_home))
-                def _():
-                    coord_remote(0, 0).start()
-            else:
-                coord_remote(j, t).start()
-
-    for k in range(1, chips):
-        block = lax.rem(chip + k, chips) * 2 + core
-        sino_copy(sino, block, mate, f_send.at[k]).wait_recv()
-        sino_copy(all_sino.at[block], block, mate, f_send.at[k]).start()
-    for k in range(chips):
-        block = lax.rem(chip + k, chips) * 2 + 1 - core
-        sino_copy(sino, block, mate, f_send.at[0]).wait_recv()
-    for g in range(groups):
+    def far(k):
+        return lax.rem(outer + k, outers) * 4 + me % 4
+
+    primary = me // share == half
+    for k in range(1, outers):
+        sino_copy(me, far(k), s_send.at[k], sino).start()
+    sino_copy(me, near, n_send.at[0], sino).start()
+    sino_copy(me, mate, f_send.at[0], sino).start()
+    for j in range(1, share):
+        place = lax.rem(me + j, share)
+        coord_copy(me, half * share + place, half, c_send.at[j], coords.at[place]).start()
+    home = lax.rem(me, share)
+
+    @pl.when(primary)
+    def _():
+        pltpu.make_async_copy(coords.at[home], all_coords.at[me], c_recv.at[me]).start()
+
+    @pl.when(jnp.logical_not(primary))
+    def _():
+        coord_copy(me, half * share + home, half, c_send.at[0], coords.at[home]).start()
+
+    def arrived(block):
+        sino_copy(block, mate, s_send.at[0]).wait_recv()
+
+    for k in range(1, outers):
+        arrived(far(k))
+        sino_copy(far(k), near, n_send.at[k]).start()
+        sino_copy(far(k), mate, f_send.at[k]).start()
+
+    def spread(g):
         pltpu.make_async_copy(coords.at[0], all_coords.at[g], c_recv.at[g]).wait()
+
+        @pl.when(primary)
+        def _():
+            for t in range(1, halves):
+                side = lax.rem(half + t, halves)
+                coord_copy(g, me, side, x_send.at[g * (halves - 1) + t - 1]).start()
+
+    def from_near(k):
+        return lax.rem(outer + k, outers) * 4 + near % 4
+
+    for k in range(outers):
+        for i in range(4):
+            spread(lax.rem(outer + k, outers) * 4 + i)
+        arrived(from_near(k))
+        sino_copy(from_near(k), mate, f_send.at[outers + k]).start()
+    for k in range(outers):
+        arrived(lax.rem(outer + k, outers) * 4 + mate % 4)
+        arrived(lax.rem(outer + k, outers) * 4 + 3 - me % 4)
     own.wait()
-    for k in range(1, chips):
-        sino_copy(sino, me, mate, s_send.at[k]).wait_send()
-    for k in range(chips):
-        sino_copy(sino, me, mate, f_send.at[k]).wait_send()
-    for j in range(share):
-        for t in range(halves):
-            if j == 0 and t == 0:
-                @pl.when(jnp.logical_not(at_home))
-                def _():
-                    coord_remote(0, 0).wait_send()
-            else:
-                coord_remote(j, t).wait_send()
+    for k in range(1, outers):
+        sino_copy(me, mate, s_send.at[k]).wait_send()
+    for k in range(outers):
+        sino_copy(me, mate, n_send.at[k]).wait_send()
+    for k in range(2 * outers):
+        sino_copy(me, mate, f_send.at[k]).wait_send()
+    for j in range(1, share):
+        coord_copy(me, mate, half, c_send.at[j]).wait_send()
+
+    @pl.when(jnp.logical_not(primary))
+    def _():
+        coord_copy(me, mate, half, c_send.at[0]).wait_send()
+
+    @pl.when(primary)
+    def _():
+        for i in range(groups * (halves - 1)):
+            coord_copy(me, mate, half, x_send.at[i]).wait_send()
 
 
 def shards(sinogram, detector_coord):
@@ -221,10 +240,12 @@
         out_specs=(vmem, vmem),
         scratch_shapes=[
             pltpu.SemaphoreType.DMA((1,)),
+            pltpu.SemaphoreType.DMA((groups // 4,)),
+            pltpu.SemaphoreType.DMA((groups // 4,)),
             pltpu.SemaphoreType.DMA((groups // 2,)),
             pltpu.SemaphoreType.DMA((groups,)),
-            pltpu.SemaphoreType.DMA((groups // 2,)),
-            pltpu.SemaphoreType.DMA((groups,)),
+            pltpu.SemaphoreType.DMA((share,)),
+            pltpu.SemaphoreType.DMA((groups * (halves - 1),)),
             pltpu.SemaphoreType.DMA((groups,)),
         ],
         compiler_params=pltpu.CompilerParams(collective_id=0, has_side_effects=True),

time: 37.7 us -> 35.4 us (0.939)
  the two profiles are of different devices: /device:TPU:0 before, /device:TPU:11 now
where the time goes in v4:
time: 35.4 us; the launch traced here: 35.2 us
  Pallas kernels  33 us (93%)
  local copies, waits for them, and re-layouts  2.15 us (6%)
    pallas_call x1, Pallas kernels, shards(): pl.pallas_call(functools.partial(exchange_kernel, groups, halves), out_sh...  19.6 us
    pallas_call x1, Pallas kernels, shards(): pl.pallas_call(functools.partial(project_kernel, own_angles), out_shape=j...  13.3 us
    reshape x1, local copies, waits for them, and re-layouts, shards(): sino = sinogram.reshape(slices * own_angles, bins)  1.42 us

profile of v4, /device:TPU:11, one launch (start us, length us, event | category | flops | bytes accessed | tf_op | source)
XLA Modules:
  0.0 35.2 jit_solution(2917762803127002873)
XLA Ops:
  0.0 0.0 copy-start
  0.0 1.4 %reshape.12.sino = bf16[16,1024]{1,0:T(8,128)(2,1)} reshape(bf16[8,2,1024]{2,1,0:T(2,128)(2,1)} %param.2) | data formatting | bytes 65536 | tf_op jit(solution)/shard_map/reshape | solution.py:229
  1.4 0.0 copy-done
  1.5 0.7 %reshape.14.coords = s32[8,16,128]{2,1,0:T(8,128)} reshape(s32[8,2,2,512]{3,2,1,0:T(2,128)S(1)} %bitcast.5) | data formatting | bytes 131072 | tf_op jit(solution)/shard_map/reshape | solution.py:231
  2.2 19.6 %shard_map.28 = (bf16[16,16,1024]{2,1,0:T(8,128)(2,1)}, s32[16,16,128]{2,1,0:T(8,128)}) custom-call(bf16[16,1024]{1,0:T(8,128)(2,1)} %reshape.12.sino, s32[8,16,128]{2,1,0:T(8,128)} %reshape.14.coords), custom_call_target="tpu_custom_call" | custom-call | tf_op jit(solution)/shard_map/pallas_call | solution.py:233
  21.8 13.3 %shard_map.29 = f32[2,8,512]{2,1,0:T(8,128)} custom-call(bf16[256,1024]{1,0:T(8,128)(2,1)} %bitcast.4, s32[16,16,128]{2,1,0:T(8,128)} %get-tuple-element.8.coords), custom_call_target="tpu_custom_call" | custom-call | tf_op jit(solution)/shard_map/pallas_call | solution.py:254
  (2 shorter events, 0.0 us)
Async XLA Ops:
  0.0 1.4 %copy-start = (s32[2,16,512]{2,1,0:T(8,128)S(1)}, s32[2,16,512]{2,1,0:T(8,128)}, u32[]{:S(2)}) copy-start(s32[2,16,512]{2,1,0:T(8,128)} %param.3) | copy-start | bytes 196612

commit v5 on v4

--- a/solution.py
+++ b/solution.py
@@ -33,13 +33,13 @@
 
 
 def filter_rows(sino, ramp, tiles, size, count):
-    rows = sino.shape[0]
-    per_row = sino.shape[1] // LANES
+    rows = sino.shape[0] * sino.shape[1]
+    per_row = sino.shape[2] // LANES
     for out_block in range(count):
         total = None
         for in_block in range(count):
             part = jnp.dot(
-                sino[:, in_block * size : (in_block + 1) * size],
+                sino[:, :, in_block * size : (in_block + 1) * size].reshape(rows, size),
                 ramp[out_block - in_block + count - 1],
                 preferred_element_type=jnp.float32,
             )
@@ -100,17 +100,8 @@
                 out[r, pl.ds(s, 1), pl.ds(x * LANES, LANES)] = line
 
 
-def project_kernel(own_angles, sino, coords, out, ramp, tiles):
-    bins = sino.shape[1]
-    size = ramp.shape[1]
-    build_ramp(ramp, size, bins // size)
-    filter_rows(sino, ramp, tiles, size, bins // size)
-    scale = jnp.float32(math.pi / (own_angles * coords.shape[0]))
-    interpolate(coords, tiles, out, scale, own_angles)
-
-
-def exchange_kernel(
-    groups, halves, sino, coords, all_sino, all_coords,
+def kernel(
+    groups, halves, own_angles, sino, coords, out, all_sino, all_coords, ramp, tiles,
     local_sem, s_send, n_send, f_send, s_recv, c_send, x_send, c_recv,
 ):
     me, half = lax.axis_index("ang"), lax.axis_index("sl")
@@ -133,6 +124,8 @@
     lax.fori_loop(1, total, greet, 0)
     own = pltpu.make_async_copy(sino, all_sino.at[me], local_sem.at[0])
     own.start()
+    bins, size = sino.shape[1], ramp.shape[1]
+    build_ramp(ramp, size, bins // size)
     pl.semaphore_wait(barrier, total - 1)
 
     def sino_copy(block, target, send_sem, source=None):
@@ -201,6 +194,9 @@
         arrived(lax.rem(outer + k, outers) * 4 + mate % 4)
         arrived(lax.rem(outer + k, outers) * 4 + 3 - me % 4)
     own.wait()
+    filter_rows(all_sino, ramp, tiles, size, bins // size)
+    scale = jnp.float32(math.pi / (own_angles * groups))
+    interpolate(all_coords, tiles, out, scale, own_angles)
     for k in range(1, outers):
         sino_copy(me, mate, s_send.at[k]).wait_send()
     for k in range(outers):
@@ -230,15 +226,17 @@
     coords = detector_coord.reshape(own_angles, share, row_share, width)
     coords = coords.transpose(1, 0, 2, 3).reshape(share, -1, LANES)
     vmem = pl.BlockSpec(memory_space=pltpu.VMEM)
-    all_sino, all_coords = pl.pallas_call(
-        functools.partial(exchange_kernel, groups, halves),
-        out_shape=(
-            jax.ShapeDtypeStruct((groups,) + sino.shape, sino.dtype),
-            jax.ShapeDtypeStruct((groups,) + coords.shape[1:], coords.dtype),
-        ),
+    size = 256
+    return pl.pallas_call(
+        functools.partial(kernel, groups, halves, own_angles),
+        out_shape=jax.ShapeDtypeStruct((row_share, slices, width), jnp.float32),
         in_specs=[vmem] * 2,
-        out_specs=(vmem, vmem),
+        out_specs=vmem,
         scratch_shapes=[
+            pltpu.VMEM((groups,) + sino.shape, sino.dtype),
+            pltpu.VMEM((groups,) + coords.shape[1:], coords.dtype),
+            pltpu.VMEM((2 * (bins // size) - 1, size, size), jnp.bfloat16),
+            pltpu.VMEM((groups * slices * own_angles * bins // LANES, LANES), jnp.float32),
             pltpu.SemaphoreType.DMA((1,)),
             pltpu.SemaphoreType.DMA((groups // 4,)),
             pltpu.SemaphoreType.DMA((groups // 4,)),
@@ -250,17 +248,6 @@
         ],
         compiler_params=pltpu.CompilerParams(collective_id=0, has_side_effects=True),
     )(sino, coords)
-    size = 256
-    return pl.pallas_call(
-        functools.partial(project_kernel, own_angles),
-        out_shape=jax.ShapeDtypeStruct((row_share, slices, width), jnp.float32),
-        in_specs=[vmem] * 2,
-        out_specs=vmem,
-        scratch_shapes=[
-            pltpu.VMEM((2 * (bins // size) - 1, size, size), jnp.bfloat16),
-            pltpu.VMEM((groups * slices * own_angles * bins // LANES, LANES), jnp.float32),
-        ],
-    )(all_sino.reshape(groups * slices * own_angles, bins), all_coords)
 
 
 def solution(mesh):

time: 35.4 us -> 34.8 us (0.983)
  Pallas kernels: 33 us -> 30.8 us
  local copies, waits for them, and re-layouts: 2.15 us -> 3.64 us
    pallas_call x2 -> x1, Pallas kernels: 33 us -> 30.8 us  [shards(): pl.pallas_call(functools.partial(kernel, groups, halves, own_angles), out...]
    unnamed x2 -> x3, local copies, waits for them, and re-layouts: 0.01 us -> 1.46 us
    reshape x2, local copies, waits for them, and re-layouts: 0.04 us -> 0.88 us  [shards(): coords = detector_coord.reshape(own_angles, share, row_share, width)]
    reshape x1, local copies, waits for them, and re-layouts: 1.42 us -> 0.63 us  [shards(): sino = sinogram.reshape(slices * own_angles, bins)]
where the time goes in v5:
time: 34.8 us; the launch traced here: 34.5 us
  Pallas kernels  30.8 us (89%)
  local copies, waits for them, and re-layouts  3.64 us (10%)
    pallas_call x1, Pallas kernels, shards(): pl.pallas_call(functools.partial(kernel, groups, halves, own_angles), out...  30.8 us
    unnamed x3, local copies, waits for them, and re-layouts  1.46 us
    reshape x2, local copies, waits for them, and re-layouts, shards(): coords = detector_coord.reshape(own_angles, share, row_share, width)  0.88 us

profile of v5, /device:TPU:11, one launch (start us, length us, event | category | flops | bytes accessed | tf_op | source)
XLA Modules:
  0.0 34.5 jit_solution(3207111968521823286)
XLA Ops:
  0.0 0.9 %reshape.10 = s32[2,8,2,512]{3,2,1,0:T(2,128)S(1)} reshape(s32[2,16,512]{2,1,0:T(8,128)} %param.3) | data formatting | bytes 131072 | tf_op jit(solution)/shard_map/reshape | solution.py:226
  0.9 0.0 copy-start
  0.9 0.7 %reshape.11.coords = s32[8,16,128]{2,1,0:T(8,128)} reshape(s32[8,2,2,512]{3,2,1,0:T(2,128)S(1)} %bitcast.3) | data formatting | bytes 131072 | tf_op jit(solution)/shard_map/reshape | solution.py:227
  1.6 0.1 copy-done
  1.7 0.6 %reshape.9.sino = bf16[16,1024]{1,0:T(8,128)(2,1)} reshape(bf16[8,2,1024]{2,1,0:T(2,128)(2,1)S(1)} %copy-done) | data formatting | bytes 65536 | tf_op jit(solution)/shard_map/reshape | solution.py:225
  2.3 30.8 %shard_map.28 = f32[2,8,512]{2,1,0:T(8,128)} custom-call(bf16[16,1024]{1,0:T(8,128)(2,1)} %reshape.9.sino, s32[8,16,128]{2,1,0:T(8,128)} %reshape.11.coords), custom_call_target="tpu_custom_call" | custom-call | tf_op jit(solution)/shard_map/pallas_call | solution.py:230
  33.1 1.4 %copy.7 = f32[2,8,512]{2,1,0:T(8,128)} copy(f32[2,8,512]{2,1,0:T(8,128)} %shard_map.28) | data formatting | bytes 65536
  (1 shorter events, 0.0 us)
Async XLA Ops:
  0.9 0.8 %copy-start = (bf16[8,2,1024]{2,1,0:T(2,128)(2,1)S(1)}, bf16[8,2,1024]{2,1,0:T(2,128)(2,1)}, u32[]{:S(2)}) copy-start(bf16[8,2,1024]{2,1,0:T(2,128)(2,1)} %param.2) | copy-start | bytes 98308

commit v6 on v5

--- a/solution.py
+++ b/solution.py
@@ -173,28 +173,39 @@
         sino_copy(far(k), near, n_send.at[k]).start()
         sino_copy(far(k), mate, f_send.at[k]).start()
 
+    def coords_arrived(g):
+        pltpu.make_async_copy(coords.at[0], all_coords.at[g], c_recv.at[g]).wait()
+
     def spread(g):
-        pltpu.make_async_copy(coords.at[0], all_coords.at[g], c_recv.at[g]).wait()
-
-        @pl.when(primary)
-        def _():
-            for t in range(1, halves):
-                side = lax.rem(half + t, halves)
-                coord_copy(g, me, side, x_send.at[g * (halves - 1) + t - 1]).start()
+        coords_arrived(g)
+        for t in range(1, halves):
+            side = lax.rem(half + t, halves)
+            coord_copy(g, me, side, x_send.at[g * (halves - 1) + t - 1]).start()
 
     def from_near(k):
         return lax.rem(outer + k, outers) * 4 + near % 4
 
     for k in range(outers):
-        for i in range(4):
-            spread(lax.rem(outer + k, outers) * 4 + i)
         arrived(from_near(k))
         sino_copy(from_near(k), mate, f_send.at[outers + k]).start()
+
+    @pl.when(primary)
+    def _():
+        for k in range(outers):
+            for i in range(4):
+                spread(lax.rem(outer + k, outers) * 4 + i)
+
     for k in range(outers):
         arrived(lax.rem(outer + k, outers) * 4 + mate % 4)
         arrived(lax.rem(outer + k, outers) * 4 + 3 - me % 4)
     own.wait()
     filter_rows(all_sino, ramp, tiles, size, bins // size)
+
+    @pl.when(jnp.logical_not(primary))
+    def _():
+        for g in range(groups):
+            coords_arrived(g)
+
     scale = jnp.float32(math.pi / (own_angles * groups))
     interpolate(all_coords, tiles, out, scale, own_angles)
     for k in range(1, outers):

time: 34.8 us -> 34.3 us (0.986)
  the two profiles are of different devices: /device:TPU:11 before, /device:TPU:10 now
where the time goes in v6:
time: 34.3 us; the launch traced here: 33.9 us
  Pallas kernels  30.3 us (88%)
  local copies, waits for them, and re-layouts  3.64 us (11%)
    pallas_call x1, Pallas kernels, shards(): pl.pallas_call(functools.partial(kernel, groups, halves, own_angles), out...  30.3 us
    unnamed x3, local copies, waits for them, and re-layouts  1.46 us
    reshape x2, local copies, waits for them, and re-layouts, shards(): coords = detector_coord.reshape(own_angles, share, row_share, width)  0.88 us

profile of v6, /device:TPU:10, one launch (start us, length us, event | category | flops | bytes accessed | tf_op | source)
XLA Modules:
  0.0 33.9 jit_solution(4327233350399226329)
XLA Ops:
  0.0 0.9 %reshape.10 = s32[2,8,2,512]{3,2,1,0:T(2,128)S(1)} reshape(s32[2,16,512]{2,1,0:T(8,128)} %param.3) | data formatting | bytes 131072 | tf_op jit(solution)/shard_map/reshape | solution.py:237
  0.9 0.0 copy-start
  0.9 0.7 %reshape.11.coords = s32[8,16,128]{2,1,0:T(8,128)} reshape(s32[8,2,2,512]{3,2,1,0:T(2,128)S(1)} %bitcast.3) | data formatting | bytes 131072 | tf_op jit(solution)/shard_map/reshape | solution.py:238
  1.6 0.1 copy-done
  1.7 0.6 %reshape.9.sino = bf16[16,1024]{1,0:T(8,128)(2,1)} reshape(bf16[8,2,1024]{2,1,0:T(2,128)(2,1)S(1)} %copy-done) | data formatting | bytes 65536 | tf_op jit(solution)/shard_map/reshape | solution.py:236
  2.3 30.3 %shard_map.28 = f32[2,8,512]{2,1,0:T(8,128)} custom-call(bf16[16,1024]{1,0:T(8,128)(2,1)} %reshape.9.sino, s32[8,16,128]{2,1,0:T(8,128)} %reshape.11.coords), custom_call_target="tpu_custom_call" | custom-call | tf_op jit(solution)/shard_map/pallas_call | solution.py:241
  32.6 1.4 %copy.7 = f32[2,8,512]{2,1,0:T(8,128)} copy(f32[2,8,512]{2,1,0:T(8,128)} %shard_map.28) | data formatting | bytes 65536
  (1 shorter events, 0.0 us)
Async XLA Ops:
  0.9 0.8 %copy-start = (bf16[8,2,1024]{2,1,0:T(2,128)(2,1)S(1)}, bf16[8,2,1024]{2,1,0:T(2,128)(2,1)}, u32[]{:S(2)}) copy-start(bf16[8,2,1024]{2,1,0:T(2,128)(2,1)} %param.2) | copy-start | bytes 98308
